TPU v7x, 32 devices: a whole 2x2x4 slice. The times are simulated.
32 devices in a mesh: dp: 4 (over y, x), row: 2 (over core), col: 4 (over z).
Axes of the slice: x: 2, y: 2, z: 4, core: 2. Of those that a mesh axis runs over, the one named last changes fastest.
Arguments:
- tokens: bfloat16 [3840, 4096], P(('dp', 'col'), 'row'), may hold values from -6 to 6
- hidden_cot: bfloat16 [3840, 14336], P(('dp', 'row'), 'col'), may hold values from -0.09667969 to 0.09667969
- gate_pre: bfloat16 [3840, 14336], P(('dp', 'row'), 'col'), may hold values from -10 to 10
- up_pre: bfloat16 [3840, 14336], P(('dp', 'row'), 'col'), may hold values from -6 to 6
Outputs:
- grad_gate: bfloat16 [2, 2048, 14336], P('row', 'dp', 'col')
All inputs are finite; a program needn't handle non-finite values.
Results may differ from a plain program's by a relative error of at most 0.014.
Values may be sent and summed in bfloat16 or wider, within the bound.
A program may use at most 128 MiB of HBM per device.

v0:
```python
import jax
import jax.numpy as jnp
from jax import lax
from jax.sharding import PartitionSpec as P


def contract_rows(left, right):
    return lax.dot_general(
        left, right, (((0,), (0,)), ((), ())), preferred_element_type=jnp.float32
    )


def on_device(tokens, hidden_cot, gate_pre, up_pre):
    tok_full = lax.all_gather(tokens, "col", axis=0, tiled=True)
    gate_val = gate_pre.astype(jnp.float32)
    up_val = up_pre.astype(jnp.float32)
    cot_val = hidden_cot.astype(jnp.float32)
    sigma = jax.nn.sigmoid(gate_val)
    gate_grad = (cot_val * up_val * sigma * (1.0 + gate_val * (1.0 - sigma))).astype(jnp.bfloat16)
    grad_full = lax.all_gather(gate_grad, "row", axis=0, tiled=True)
    group_part = contract_rows(tok_full, grad_full)
    summed = lax.psum_scatter(
        group_part.astype(jnp.bfloat16), "dp", scatter_dimension=0, tiled=True
    )
    return summed.reshape(1, summed.shape[0], summed.shape[1])


def solution(mesh):
    in_specs = (
        P(("dp", "col"), "row"),
        P(("dp", "row"), "col"),
        P(("dp", "row"), "col"),
        P(("dp", "row"), "col"),
    )
    out_specs = P("row", "dp", "col")
    return jax.shard_map(
        on_device, mesh=mesh, in_specs=in_specs, out_specs=out_specs, check_vma=False
    )
```

profile of v0, /device:TPU:0, one launch (start us, length us, event | category | flops | bytes accessed | tf_op | source)
XLA Modules:
  0.0 279.2 jit_solution(14229257457182751783)
XLA Ops:
  6.5 0.0 all-gather.5.cloned.1.call-start
  6.5 0.7 all-gather.5.cloned.1.call-update
  7.3 0.0 all-gather.3.cloned.1.call-start
  7.3 6.7 %fusion.6 = bf16[480,3584]{1,0:T(8,128)(2,1)} fusion(bf16[480,3584]{1,0:T(8,128)(2,1)} %param.6, bf16[480,3584]{1,0:T(8,128)(2,1)} %param.7, bf16[480,3584]{1,0:T(8,128)(2,1)} %param.5), kind=kLoop, calls=%fused_computation.9 | loop fusion | flops 22364160 | bytes 13762560 | tf_op jit(solution)/shard_map/convert_element_type | solution.py:19
  14.0 0.0 all-gather.3.cloned.1.call-update
  14.1 0.0 reduce-scatter.2.cloned.1.call-start
  14.1 74.0 %all-gather.5.cloned.1.call-done = bf16[960,2048]{1,0:T(8,128)(2,1)} async-done(((bf16[240,2048]{1,0:T(8,128)(2,1)}), bf16[960,2048]{1,0:T(8,128)(2,1)}) %all-gather.5.cloned.1.call-update) | async-done | bytes 3932176 | tf_op jit(solution)/shard_map/all_gather | solution.py:14
  88.1 17.7 %all-gather.3.cloned.1.call-done = bf16[960,3584]{1,0:T(8,128)(2,1)} async-done(((bf16[480,3584]{1,0:T(8,128)(2,1)}), bf16[960,3584]{1,0:T(8,128)(2,1)}) %all-gather.3.cloned.1.call-update) | async-done | bytes 6881296 | tf_op jit(solution)/shard_map/all_gather | solution.py:20
  105.8 21.9 %fusion = bf16[2048,3584]{0,1:T(8,128)(2,1)} fusion(bf16[960,3584]{1,0:T(8,128)(2,1)} %all-gather.3.cloned.1.call-done, bf16[960,2048]{1,0:T(8,128)(2,1)} %all-gather.5.cloned.1.call-done), kind=kOutput, calls=%fused_computation.1 | convolution fusion | flops 14100201472 | bytes 25493504 | tf_op jit(solution)/shard_map/dot_general | solution.py:8
  127.7 0.0 reduce-scatter.2.cloned.1.call-update
  127.7 139.1 %reduce-scatter.2.cloned.1.call-done = bf16[512,3584]{0,1:T(8,128)(2,1)} async-done(((bf16[2048,3584]{0,1:T(8,128)(2,1)}), bf16[512,3584]{0,1:T(8,128)(2,1)}) %reduce-scatter.2.cloned.1.call-update) | async-done | bytes 3670032 | tf_op jit(solution)/shard_map/reduce_scatter | solution.py:22
  266.8 5.9 %copy.5 = bf16[1,512,3584]{2,1,0:T(8,128)(2,1)} copy(bf16[1,512,3584]{1,2,0:T(8,128)(2,1)} %bitcast.5) | data formatting | bytes 7340032 | tf_op jit(solution)/shard_map/reshape | solution.py:25
Async XLA Ops:
  6.5 81.5 %all-gather.5.cloned.1.call-start = ((), (), s32[]{:S(2)}) async-start(), calls=%async_computation.2 | async-start | bytes 4915200 | tf_op jit(solution)/shard_map/all_gather | solution.py:14
  7.3 98.5 %all-gather.3.cloned.1.call-start = ((), (), s32[]{:S(2)}) async-start(), calls=%async_computation.1 | async-start | bytes 10321920 | tf_op jit(solution)/shard_map/all_gather | solution.py:20
  14.1 252.7 %reduce-scatter.2.cloned.1.call-start = ((), (), s32[]{:S(2)}) async-start(), calls=%async_computation.3 | async-start | bytes 18350080 | tf_op jit(solution)/shard_map/reduce_scatter | solution.py:22
Sparse Core Ops, SparseCore 0:
  8.9 79.1 all-gather.4
  89.6 16.1 all-gather.2
  127.8 138.9 reduce-scatter.1
where the time goes:
time: 279 us
  waiting for transfers between devices  232 us (83%)
  matrix products  21.9 us (8%)
  between operations  13.1 us (5%)
  other arithmetic  6.73 us (2%)
  local copies, waits for them, and re-layouts  5.91 us (2%)
    reduce_scatter x1, waiting for transfers between devices, on_device(): lax.psum_scatter(group_part.astype(jnp.bfloat16), 'dp', scatter_dimension...  139 us
    all_gather x1, waiting for transfers between devices, on_device(): tok_full = lax.all_gather(tokens, 'col', axis=0, tiled=True)  74 us
    dot_general x1, matrix products, contract_rows(): lax.dot_general(left, right, (((0,), (0,)), ((), ())), preferred_element_...  21.9 us
    all_gather x1, waiting for transfers between devices, on_device(): grad_full = lax.all_gather(gate_grad, 'row', axis=0, tiled=True)  17.7 us
    convert_element_type x1, other arithmetic, on_device(): (cot_val * up_val * sigma * (1.0 + gate_val * (1.0 - sigma))).astype(jnp....  6.73 us
    reshape x1, local copies, waits for them, and re-layouts, on_device(): return summed.reshape(1, summed.shape[0], summed.shape[1])  5.91 us
  transfers between devices with their start and end apart: 3, of which 3 were waited for; matrix products, arithmetic and copies ran while one was open for 2% of the time, Pallas kernels for 0%

commit v1 on v0

v1 whole, which is shorter than its diff:
```python
import functools
import math

import jax
import jax.numpy as jnp
from jax import lax
from jax.experimental import pallas as pl
from jax.experimental.pallas import tpu as pltpu
from jax.sharding import PartitionSpec as P

MESH = pl.DeviceIdType.MESH


def near_square(n):
    nx = math.isqrt(n)
    while n % nx:
        nx -= 1
    return n // nx, nx


def kernel(dims, starts, tok, cot, gate, up, out, ins, grads, toks, tokt, part, got, res,
           in_sem, own_sem, ty_s, ty_r, tz_s, tz_r, gy_s, gy_r, gp_s, gp_r, x_s, x_r, out_sem):
    ny, nx, nr, nz, wide, block, chunks, cols = dims
    dp, r, z = lax.axis_index("dp"), lax.axis_index("row"), lax.axis_index("col")
    y, x = dp // nx, dp % nx
    subs = wide // block
    away = (nx - 1) * subs
    blocks = nx * subs
    rows = ny * nr * grads.shape[3]

    def at(oy=0, ox=0, orow=0, oz=0):
        return {
            "dp": (y + oy) % ny * nx + (x + ox) % nx,
            "row": (r + orow) % nr,
            "col": (z + oz) % nz,
        }

    def remote(src, dst, ss, rs, to):
        return pltpu.make_async_remote_copy(
            src_ref=src, dst_ref=dst, send_sem=ss, recv_sem=rs, device_id=to, device_id_type=MESH)

    def each(n, f):
        def body(i, c):
            f(i)
            return c
        lax.fori_loop(0, n, body, 0)

    def load(k, i):
        src = (cot, gate, up)[i]
        return pltpu.make_async_copy(
            src.at[:, pl.ds(pl.multiple_of(k * cols, cols), cols)], ins.at[i, k], in_sem.at[i, k])

    def tok_cols(oy, b):
        o, sub = (b // subs + 1) % nx, b % subs
        first = ((y + oy) % ny * nx + (x + o) % nx) * wide + sub * block
        return tok.at[:, pl.ds(pl.multiple_of(first, block), block)]

    def own_tok(b):
        return pltpu.make_async_copy(tok_cols(0, b), toks.at[b, y, z], own_sem.at[b])

    def tok_y(oy, b):
        return remote(tok_cols(oy, b), toks.at[b, y, z], ty_s.at[oy - 1, b], ty_r.at[oy - 1, b], at(oy=oy))

    def tok_z(oz, b, oy):
        ref = toks.at[b, (y - oy + ny) % ny, z]
        return remote(ref, ref, tz_s.at[oz - 1, b, oy], tz_r.at[oz - 1, b, oy], at(oz=oz))

    def grad_y(oy, k):
        ref = grads.at[k, y, r]
        return remote(ref, ref, gy_s.at[oy - 1, k], gy_r.at[oy - 1, k], at(oy=oy))

    def grad_p(orow, oy, k):
        ref = grads.at[k, (y - oy + ny) % ny, r]
        return remote(ref, ref, gp_s.at[orow - 1, oy, k], gp_r.at[orow - 1, oy, k], at(orow=orow))

    def sum_x(b, k):
        return remote(part.at[b, k], got.at[b, k], x_s.at[b, k], x_r.at[b, k], at(ox=b // subs + 1))

    def write(sub, k):
        return pltpu.make_async_copy(
            res.at[sub, k],
            out.at[0, pl.ds(sub * block, block), pl.ds(pl.multiple_of(k * cols, cols), cols)],
            out_sem.at[sub, k])

    for b in range(blocks):
        own_tok(b).start()

    def load_all(k):
        for i in range(3):
            load(k, i).start()
    each(chunks, load_all)

    peers = ([at(oy=o) for o in range(1, ny)] + [at(ox=o) for o in range(1, nx)]
             + [at(orow=o) for o in range(1, nr)] + [at(oz=o) for o in range(1, nz)])
    barrier = pltpu.get_barrier_semaphore()
    for to in peers:
        pl.semaphore_signal(barrier, inc=1, device_id=to, device_id_type=MESH)
    pl.semaphore_wait(barrier, len(peers))

    for b in range(blocks):
        for oy in range(1, ny):
            tok_y(oy, b).start()

    def own_out(b):
        own_tok(b).wait()
        for oz in range(1, nz):
            tok_z(oz, b, 0).start()

    def pass_on(b):
        for oy in range(1, ny):
            tok_y(oy, b).wait_recv()
            for oz in range(1, nz):
                tok_z(oz, b, oy).start()

    def gate_grad(k):
        for i in range(3):
            load(k, i).wait()
        step = 32
        tall = ins.shape[2]

        def rows_of(j, c):
            at_rows = pl.ds(pl.multiple_of(j * step, step), step)
            h = ins[0, k, at_rows, :].astype(jnp.float32)
            g = ins[1, k, at_rows, :].astype(jnp.float32)
            u = ins[2, k, at_rows, :].astype(jnp.float32)
            s = jax.nn.sigmoid(g)
            grads[k, y, r, at_rows, :] = (h * u * s * (1.0 + g * (1.0 - s))).astype(grads.dtype)
            return c
        lax.fori_loop(0, tall // step, rows_of, 0)
        for oy in range(1, ny):
            grad_y(oy, k).start()
        for orow in range(1, nr):
            grad_p(orow, 0, k).start()

    for b in range(away):
        own_out(b)
    early = min(4, chunks)
    each(early, gate_grad)
    for b in range(away):
        pass_on(b)
    for b in range(away, blocks):
        own_out(b)
    each(chunks - early, lambda k: gate_grad(k + early))
    for b in range(away, blocks):
        pass_on(b)

    def arrive(k):
        for oy in range(1, ny):
            grad_y(oy, k).wait_recv()
            for orow in range(1, nr):
                grad_p(orow, oy, k).start()
        for orow in range(1, nr):
            for oy in range(ny):
                grad_p(orow, oy, k).wait_recv()

    def take_block(b):
        for oz in range(1, nz):
            for oy in range(ny):
                tok_z(oz, b, oy).wait_recv()
        tokt[b] = toks[b].reshape(rows, block).T

    def product(b, k):
        return jnp.dot(tokt[b], grads[k].reshape(rows, cols), preferred_element_type=jnp.float32)

    def tile(b, k):
        part[b, k] = product(b, k).astype(part.dtype)
        sum_x(b, k).start()

    begins = [min(starts[min(b, len(starts) - 1)], chunks - 1) for b in range(away)]
    live, done = [], 0
    for now in sorted(set(begins)) + [chunks]:
        def stretch(i, live=tuple(live), done=done):
            arrive(i + done)
            for b in live:
                tile(b, i + done)
        if now > done:
            each(now - done, stretch)
        done = now
        for b in range(away):
            if now < chunks and begins[b] == now:
                take_block(b)
                if now:
                    each(now, functools.partial(tile, b))
                live.append(b)

    for b in range(away, blocks):
        take_block(b)

    def finish(k):
        for sub in range(subs):
            total = product(away + sub, k)
            for o in range(1, nx):
                b = (o - 1) * subs + sub
                sum_x(b, k).wait_recv()
                total = total + got[b, k].astype(jnp.float32)
            res[sub, k] = total.astype(res.dtype)
            write(sub, k).start()
    each(chunks, finish)

    for b in range(blocks):
        for oy in range(1, ny):
            tok_y(oy, b).wait_send()
        for oz in range(1, nz):
            for oy in range(ny):
                tok_z(oz, b, oy).wait_send()

    def drain(k):
        for oy in range(1, ny):
            grad_y(oy, k).wait_send()
        for orow in range(1, nr):
            for oy in range(ny):
                grad_p(orow, oy, k).wait_send()
        for b in range(away):
            sum_x(b, k).wait_send()
        for sub in range(subs):
            write(sub, k).wait()
    each(chunks, drain)


def solution(mesh):
    ndp, nr, nz = mesh.shape["dp"], mesh.shape["row"], mesh.shape["col"]
    ny, nx = near_square(ndp)

    def on_device(tokens, hidden_cot, gate_pre, up_pre):
        tok_rows, wid = tokens.shape
        tall, hidden = gate_pre.shape
        wide = wid // ndp
        block = math.gcd(wide, 256)
        cols = math.gcd(hidden, 256)
        chunks = hidden // cols
        subs = wide // block
        blocks, away = nx * subs, (nx - 1) * subs
        rows = ny * nz * tok_rows
        dims = (ny, nx, nr, nz, wide, block, chunks, cols)
        starts = (2, 6)
        dma = pltpu.SemaphoreType.DMA
        dt = tokens.dtype
        return pl.pallas_call(
            functools.partial(kernel, dims, starts),
            out_shape=jax.ShapeDtypeStruct((1, wide, hidden), dt),
            in_specs=[pl.BlockSpec(memory_space=pl.ANY)] * 4,
            out_specs=pl.BlockSpec(memory_space=pl.ANY),
            scratch_shapes=[
                pltpu.VMEM((3, chunks, tall, cols), dt),
                pltpu.VMEM((chunks, ny, nr, tall, cols), dt),
                pltpu.VMEM((blocks, ny, nz, tok_rows, block), dt),
                pltpu.VMEM((blocks, block, rows), dt),
                pltpu.VMEM((max(away, 1), chunks, block, cols), dt),
                pltpu.VMEM((max(away, 1), chunks, block, cols), dt),
                pltpu.VMEM((subs, chunks, block, cols), dt),
                dma((3, chunks)),
                dma((blocks,)),
                dma((max(ny - 1, 1), blocks)),
                dma((max(ny - 1, 1), blocks)),
                dma((max(nz - 1, 1), blocks, ny)),
                dma((max(nz - 1, 1), blocks, ny)),
                dma((max(ny - 1, 1), chunks)),
                dma((max(ny - 1, 1), chunks)),
                dma((max(nr - 1, 1), ny, chunks)),
                dma((max(nr - 1, 1), ny, chunks)),
                dma((max(away, 1), chunks)),
                dma((max(away, 1), chunks)),
                dma((subs, chunks)),
            ],
            compiler_params=pltpu.CompilerParams(
                collective_id=0, has_side_effects=True, vmem_limit_bytes=63 * 1024 * 1024
            ),
        )(tokens, hidden_cot, gate_pre, up_pre)

    in_specs = (
        P(("dp", "col"), "row"),
        P(("dp", "row"), "col"),
        P(("dp", "row"), "col"),
        P(("dp", "row"), "col"),
    )
    return jax.shard_map(
        on_device, mesh=mesh, in_specs=in_specs, out_specs=P("row", "dp", "col"), check_vma=False
    )
```

time: 279 us -> 141 us (0.51)
  the two profiles are of different devices: /device:TPU:0 before, /device:TPU:8 now
where the time goes in v1:
time: 141 us
  Pallas kernels  137 us (97%)
  local copies, waits for them, and re-layouts  4.11 us (3%)
    pallas_call x1, Pallas kernels, on_device(): pl.pallas_call(functools.partial(kernel, dims, starts), out_shape=jax.Sha...  137 us
    unnamed x1, local copies, waits for them, and re-layouts  4.11 us

profile of v1, /device:TPU:8, one launch (start us, length us, event | category | flops | bytes accessed | tf_op | source)
XLA Modules:
  0.0 140.7 jit_solution(13507245301603219173)
XLA Ops:
  0.0 136.5 %shard_map.46 = bf16[1,512,3584]{2,1,0:T(8,128)(2,1)} custom-call(bf16[240,2048]{1,0:T(8,128)(2,1)} %tok.1, bf16[480,3584]{1,0:T(8,128)(2,1)} %cot.1, bf16[480,3584]{1,0:T(8,128)(2,1)} %gate.1, bf16[480,3584]{1,0:T(8,128)(2,1)} %up.1), custom_call_target="tpu_custom_call" | custom-call | tf_op jit(solution)/shard_map/pallas_call | solution.py:238
  136.5 4.1 %copy.6 = bf16[1,512,3584]{2,1,0:T(8,128)(2,1)} copy(bf16[1,512,3584]{2,1,0:T(8,128)(2,1)} %shard_map.46) | data formatting | bytes 7340032

commit v2 on v1

--- a/solution.py
+++ b/solution.py
@@ -18,9 +18,10 @@
     return n // nx, nx
 
 
-def kernel(dims, starts, tok, cot, gate, up, out, ins, grads, toks, tokt, part, got, res,
+def kernel(dims, plan, tok, cot, gate, up, out, ins, grads, toks, tokt, part, got, res,
            in_sem, own_sem, ty_s, ty_r, tz_s, tz_r, gy_s, gy_r, gp_s, gp_r, x_s, x_r, out_sem):
     ny, nx, nr, nz, wide, block, chunks, cols = dims
+    ahead, own_at = plan
     dp, r, z = lax.axis_index("dp"), lax.axis_index("row"), lax.axis_index("col")
     y, x = dp // nx, dp % nx
     subs = wide // block
@@ -61,9 +62,50 @@
     def tok_y(oy, b):
         return remote(tok_cols(oy, b), toks.at[b, y, z], ty_s.at[oy - 1, b], ty_r.at[oy - 1, b], at(oy=oy))
 
-    def tok_z(oz, b, oy):
-        ref = toks.at[b, (y - oy + ny) % ny, z]
-        return remote(ref, ref, tz_s.at[oz - 1, b, oy], tz_r.at[oz - 1, b, oy], at(oz=oz))
+    reach = min(2, nz - 1)
+    hops = ([(d, 0) for d in range(1, reach + 1)] + [(1, d) for d in range(2, nz - 1)])
+
+    def valid(way, far, back):
+        left = z >= back if way > 0 else z + back < nz
+        right = z + far < nz if way > 0 else z >= far
+        return jnp.logical_and(left, right)
+
+    def tok_z(b, oy, way, i):
+        far, back = hops[i]
+        zs = z - way * back
+        ref = toks.at[b, (y - oy + ny) % ny, zs]
+        w = 0 if way > 0 else 1
+        return remote(ref, ref, tz_s.at[w, i, b, oy], tz_r.at[zs, b, oy], at(oz=way * far + nz))
+
+    def send_z(b, oy, relay, act):
+        for way in (1, -1):
+            for i, (far, back) in enumerate(hops):
+                if (back > 0) == relay:
+                    pl.when(valid(way, far, back))(functools.partial(lambda w, n: act(tok_z(b, oy, w, n)), way, i))
+
+    def got_z(b, oy, zs):
+        ref = toks.at[b, (y - oy + ny) % ny, zs]
+        return remote(ref, ref, tz_s.at[0, 0, b, oy], tz_r.at[zs, b, oy], at(oz=1))
+
+    def relay_z(b):
+        for oy in range(ny):
+            for way in (1, -1):
+                for i, (far, back) in enumerate(hops):
+                    if back:
+                        def go(way=way, i=i, back=back, oy=oy):
+                            got_z(b, oy, z - way * back).wait_recv()
+                            tok_z(b, oy, way, i).start()
+                        pl.when(valid(way, far, back))(go)
+
+    def all_z(b):
+        for oy in range(ny):
+            for zs in range(nz):
+                seen = jnp.bool_(False)
+                for way in (1, -1):
+                    for far, back in hops:
+                        if back:
+                            seen = jnp.logical_or(seen, jnp.logical_and(valid(way, far, back), z - way * back == zs))
+                pl.when(jnp.logical_and(z != zs, jnp.logical_not(seen)))(got_z(b, oy, zs).wait_recv)
 
     def grad_y(oy, k):
         ref = grads.at[k, y, r]
@@ -97,20 +139,18 @@
         pl.semaphore_signal(barrier, inc=1, device_id=to, device_id_type=MESH)
     pl.semaphore_wait(barrier, len(peers))
 
-    for b in range(blocks):
+    def tok_out(b):
         for oy in range(1, ny):
             tok_y(oy, b).start()
 
     def own_out(b):
         own_tok(b).wait()
-        for oz in range(1, nz):
-            tok_z(oz, b, 0).start()
+        send_z(b, 0, False, lambda c: c.start())
 
     def pass_on(b):
         for oy in range(1, ny):
             tok_y(oy, b).wait_recv()
-            for oz in range(1, nz):
-                tok_z(oz, b, oy).start()
+            send_z(b, oy, False, lambda c: c.start())
 
     def gate_grad(k):
         for i in range(3):
@@ -132,77 +172,94 @@
         for orow in range(1, nr):
             grad_p(orow, 0, k).start()
 
-    for b in range(away):
+    def feed(k):
+        gate_grad(k)
+        pl.when(k + lead < blocks)(lambda: tok_out(k + lead))
+
+    def take_block(b):
+        all_z(b)
+        first = pl.multiple_of(b * block, block)
+        tokt[pl.ds(first, block), :] = toks[b].reshape(rows, block).T
+
+    def tile(b, k):
+        left = tokt[pl.ds(pl.multiple_of(b * block, block), block), :]
+        right = grads[k].reshape(rows, cols)
+        part[b, k] = jnp.dot(left, right, preferred_element_type=jnp.float32).astype(part.dtype)
+        sum_x(b, k).start()
+
+    def finish(k):
+        left = tokt[away * block:, :]
+        total = jnp.dot(left, grads[k].reshape(rows, cols), preferred_element_type=jnp.float32)
+        for sub in range(subs):
+            sums = total[sub * block:(sub + 1) * block]
+            for o in range(1, nx):
+                b = (o - 1) * subs + sub
+                sum_x(b, k).wait_recv()
+                sums = sums + got[b, k].astype(jnp.float32)
+            res[sub, k] = sums.astype(res.dtype)
+            write(sub, k).start()
+
+    def span(low, high, f):
+        def body(i, c):
+            f(i)
+            return c
+        lax.fori_loop(low, high, body, 0)
+
+    def z_out(b):
         own_out(b)
-    early = min(4, chunks)
-    each(early, gate_grad)
-    for b in range(away):
         pass_on(b)
-    for b in range(away, blocks):
+
+    def z_step(j):
+        relay_z(j)
+        pl.when(j + lead < blocks)(lambda: z_out(j + lead))
+
+    relayed = lambda k: jnp.where(k >= own_at, blocks, jnp.minimum((2 * k + 5) * blocks // 24, blocks))
+    ready = lambda k: jnp.where(k >= own_at, away, jnp.minimum((2 * k + 3) * away // 12, away))
+    ended = lambda k: jnp.clip((k - own_at + 1) * 3, 0, chunks - 3)
+
+    lead = min(2, blocks)
+    for b in range(lead):
+        tok_out(b)
+    for b in range(lead):
         own_out(b)
-    each(chunks - early, lambda k: gate_grad(k + early))
-    for b in range(away, blocks):
+    for b in range(lead):
+        feed(b)
         pass_on(b)
-
-    def arrive(k):
+    span(lead, ahead, feed)
+
+    def main(k, c):
+        pl.when(k + ahead < chunks)(lambda: feed(k + ahead))
+        span(jnp.where(k > 0, relayed(k - 1), 0), relayed(k), z_step)
         for oy in range(1, ny):
             grad_y(oy, k).wait_recv()
             for orow in range(1, nr):
                 grad_p(orow, oy, k).start()
+
+        def catch_up(b):
+            take_block(b)
+            span(0, k, functools.partial(tile, b))
+        now = ready(k)
+        span(jnp.where(k > 0, ready(k - 1), 0), now, catch_up)
+
+        @pl.when(k == own_at)
+        def _():
+            span(away, blocks, take_block)
+        span(ended(k - 1), ended(k), finish)
         for orow in range(1, nr):
             for oy in range(ny):
                 grad_p(orow, oy, k).wait_recv()
-
-    def take_block(b):
-        for oz in range(1, nz):
-            for oy in range(ny):
-                tok_z(oz, b, oy).wait_recv()
-        tokt[b] = toks[b].reshape(rows, block).T
-
-    def product(b, k):
-        return jnp.dot(tokt[b], grads[k].reshape(rows, cols), preferred_element_type=jnp.float32)
-
-    def tile(b, k):
-        part[b, k] = product(b, k).astype(part.dtype)
-        sum_x(b, k).start()
-
-    begins = [min(starts[min(b, len(starts) - 1)], chunks - 1) for b in range(away)]
-    live, done = [], 0
-    for now in sorted(set(begins)) + [chunks]:
-        def stretch(i, live=tuple(live), done=done):
-            arrive(i + done)
-            for b in live:
-                tile(b, i + done)
-        if now > done:
-            each(now - done, stretch)
-        done = now
-        for b in range(away):
-            if now < chunks and begins[b] == now:
-                take_block(b)
-                if now:
-                    each(now, functools.partial(tile, b))
-                live.append(b)
-
-    for b in range(away, blocks):
-        take_block(b)
-
-    def finish(k):
-        for sub in range(subs):
-            total = product(away + sub, k)
-            for o in range(1, nx):
-                b = (o - 1) * subs + sub
-                sum_x(b, k).wait_recv()
-                total = total + got[b, k].astype(jnp.float32)
-            res[sub, k] = total.astype(res.dtype)
-            write(sub, k).start()
-    each(chunks, finish)
-
-    for b in range(blocks):
+        span(0, now, lambda b: tile(b, k))
+        return c
+    lax.fori_loop(0, chunks, main, 0)
+    span(ended(chunks - 1), chunks, finish)
+
+    def done(b):
         for oy in range(1, ny):
             tok_y(oy, b).wait_send()
-        for oz in range(1, nz):
-            for oy in range(ny):
-                tok_z(oz, b, oy).wait_send()
+        for oy in range(ny):
+            for relay in (False, True):
+                send_z(b, oy, relay, lambda c: c.wait_send())
+    each(blocks, done)
 
     def drain(k):
         for oy in range(1, ny):
@@ -225,18 +282,18 @@
         tok_rows, wid = tokens.shape
         tall, hidden = gate_pre.shape
         wide = wid // ndp
-        block = math.gcd(wide, 256)
+        block = math.gcd(wide, 128)
         cols = math.gcd(hidden, 256)
         chunks = hidden // cols
         subs = wide // block
         blocks, away = nx * subs, (nx - 1) * subs
         rows = ny * nz * tok_rows
         dims = (ny, nx, nr, nz, wide, block, chunks, cols)
-        starts = (2, 6)
+        plan = (min(8, chunks), max(chunks - 5, 0))
         dma = pltpu.SemaphoreType.DMA
         dt = tokens.dtype
         return pl.pallas_call(
-            functools.partial(kernel, dims, starts),
+            functools.partial(kernel, dims, plan),
             out_shape=jax.ShapeDtypeStruct((1, wide, hidden), dt),
             in_specs=[pl.BlockSpec(memory_space=pl.ANY)] * 4,
             out_specs=pl.BlockSpec(memory_space=pl.ANY),
@@ -244,7 +301,7 @@
                 pltpu.VMEM((3, chunks, tall, cols), dt),
                 pltpu.VMEM((chunks, ny, nr, tall, cols), dt),
                 pltpu.VMEM((blocks, ny, nz, tok_rows, block), dt),
-                pltpu.VMEM((blocks, block, rows), dt),
+                pltpu.VMEM((blocks * block, rows), dt),
                 pltpu.VMEM((max(away, 1), chunks, block, cols), dt),
                 pltpu.VMEM((max(away, 1), chunks, block, cols), dt),
                 pltpu.VMEM((subs, chunks, block, cols), dt),
@@ -252,8 +309,8 @@
                 dma((blocks,)),
                 dma((max(ny - 1, 1), blocks)),
                 dma((max(ny - 1, 1), blocks)),
-                dma((max(nz - 1, 1), blocks, ny)),
-                dma((max(nz - 1, 1), blocks, ny)),
+                dma((2, max(2 * nz, 1), blocks, ny)),
+                dma((nz, blocks, ny)),
                 dma((max(ny - 1, 1), chunks)),
                 dma((max(ny - 1, 1), chunks)),
                 dma((max(nr - 1, 1), ny, chunks)),

time: 141 us -> 120 us (0.85)
  the two profiles are of different devices: /device:TPU:8 before, /device:TPU:0 now
where the time goes in v2:
time: 120 us; the launch traced here: 119 us
  Pallas kernels  115 us (96%)
  local copies, waits for them, and re-layouts  4.11 us (3%)
    pallas_call x1, Pallas kernels, on_device(): pl.pallas_call(functools.partial(kernel, dims, plan), out_shape=jax.Shape...  115 us
    unnamed x1, local copies, waits for them, and re-layouts  4.11 us

profile of v2, /device:TPU:0, one launch (start us, length us, event | category | flops | bytes accessed | tf_op | source)
XLA Modules:
  0.0 119.4 jit_solution(9104257669989552977)
XLA Ops:
  0.0 115.3 %shard_map.46 = bf16[1,512,3584]{2,1,0:T(8,128)(2,1)} custom-call(bf16[240,2048]{1,0:T(8,128)(2,1)} %tok.1, bf16[480,3584]{1,0:T(8,128)(2,1)} %cot.1, bf16[480,3584]{1,0:T(8,128)(2,1)} %gate.1, bf16[480,3584]{1,0:T(8,128)(2,1)} %up.1), custom_call_target="tpu_custom_call" | custom-call | tf_op jit(solution)/shard_map/pallas_call | solution.py:295
  115.3 4.1 %copy.6 = bf16[1,512,3584]{2,1,0:T(8,128)(2,1)} copy(bf16[1,512,3584]{2,1,0:T(8,128)(2,1)} %shard_map.46) | data formatting | bytes 7340032
